TPU v7x, 512 devices: a whole 4x8x8 slice. The times are simulated.
512 devices in a mesh: dp: 32 (over x, y), tensor: 16 (over z, core).
Axes of the slice: x: 4, y: 8, z: 8, core: 2. Of those that a mesh axis runs over, the one named last changes fastest.
Arguments:
- queries: bfloat16 [4096, 16384], P('dp', 'tensor'), may hold values from -24 to 24
- draft_keys: bfloat16 [4096, 1024], P('dp'), may hold values from -6 to 6
- draft_values: bfloat16 [4096, 1024], P('dp'), may hold values from -6 to 6
- cache_keys: bfloat16 [64, 2048, 1024], P('dp', 'tensor'), may hold values from -24 to 24
- cache_values: bfloat16 [64, 2048, 1024], P('dp', 'tensor'), may hold values from -6 to 6
- out_weight: bfloat16 [16384, 16384], P('tensor', 'dp'), may hold values from -0.25 to 0.25
- cache_lengths: int32 [64], P('dp'), may hold values from 512 to 2048
- draft_lengths: int32 [64], replicated, may hold values from 8 to 64
- dest_group: int32 [64], replicated, may hold values from 0 to 31, as said below
- dest_offset: int32 [64], replicated, may hold values from 0 to 32, as said below
Outputs:
- verified: bfloat16 [3072, 16384], P('tensor', 'dp')
Inputs may be any that keep to these rules, and one draw needn't show every extreme that they name: `dest_group`: at most one request of a group has another group as destination, and each group receives at most one such request. `dest_offset`: blocks with the same destination never intersect and end at packed row 96 or before; a block moved to another group starts right after that group's own rows; in every draw some group's blocks fill all 96 rows.
All inputs are finite; a program needn't handle non-finite values.
Results may differ from a plain program's by a relative error of at most 0.017.
Values may be sent and summed in bfloat16 or wider, within the bound.
No kernel may reach another device: no remote copies, remote signals or barrier semaphores. Data moves between devices by JAX's collectives and lax.ppermute only.
A program may use at most 64 MiB of HBM per device.

v0:
```python
import jax
import jax.numpy as jnp
from jax import lax
from jax.sharding import PartitionSpec as P

HEADS = 128
KV_HEADS = 8
HEAD_DIM = 128
DRAFT = 64
GROUP_REQ = 2
PACK = 96
NEG_FILL = -1e30


def packed_sources(row_ids, draft_lengths, dest_group, dest_offset):
    request_ids = jnp.arange(dest_group.shape[0], dtype=jnp.int32)
    slot_group = row_ids // PACK
    slot_index = row_ids % PACK
    inside = (
        (dest_group[None, :] == slot_group[:, None])
        & (slot_index[:, None] >= dest_offset[None, :])
        & (slot_index[:, None] < (dest_offset + draft_lengths)[None, :])
    )
    request = jnp.sum(jnp.where(inside, request_ids[None, :], 0), axis=1)
    first_slot = jnp.sum(jnp.where(inside, dest_offset[None, :], 0), axis=1)
    return (request, slot_index - first_slot, jnp.any(inside, axis=1))


def attend_one(operands):
    queries_one, cache_k, cache_v, draft_k, draft_v, cache_len, draft_len = operands
    score_scale = HEAD_DIM ** (-0.5)
    cache_scores = (
        jnp.einsum("qkgd,lkd->kgql", queries_one, cache_k, preferred_element_type=jnp.float32)
        * score_scale
    )
    draft_scores = (
        jnp.einsum("qkgd,jkd->kgqj", queries_one, draft_k, preferred_element_type=jnp.float32)
        * score_scale
    )
    cache_pos = jnp.arange(cache_k.shape[0], dtype=jnp.int32)
    draft_pos = jnp.arange(draft_k.shape[0], dtype=jnp.int32)
    keep_cache = cache_pos < cache_len
    keep_draft = (draft_pos[None, :] <= draft_pos[:, None]) & (draft_pos[None, :] < draft_len)
    cache_scores = jnp.where(keep_cache, cache_scores, NEG_FILL)
    draft_scores = jnp.where(keep_draft, draft_scores, NEG_FILL)
    highest = jnp.maximum(
        jnp.max(cache_scores, axis=-1, keepdims=True), jnp.max(draft_scores, axis=-1, keepdims=True)
    )
    cache_exp = jnp.exp(cache_scores - highest)
    draft_exp = jnp.exp(draft_scores - highest)
    denominator = jnp.sum(cache_exp, axis=-1, keepdims=True) + jnp.sum(
        draft_exp, axis=-1, keepdims=True
    )
    cache_weights = (cache_exp / denominator).astype(jnp.bfloat16)
    draft_weights = (draft_exp / denominator).astype(jnp.bfloat16)
    mixed = jnp.einsum("kgql,lkd->qkgd", cache_weights, cache_v, preferred_element_type=jnp.float32)
    mixed = mixed + jnp.einsum(
        "kgqj,jkd->qkgd", draft_weights, draft_v, preferred_element_type=jnp.float32
    )
    is_live = draft_pos < draft_len
    return jnp.where(is_live[:, None, None, None], mixed, 0.0).astype(jnp.bfloat16)


def body(
    queries,
    draft_keys,
    draft_values,
    cache_keys,
    cache_values,
    out_weight,
    cache_lengths,
    draft_lengths,
    dest_group,
    dest_offset,
):
    tensor_count = lax.axis_size("tensor")
    data_count = lax.axis_size("dp")
    my_rank = lax.axis_index("tensor")
    my_group = lax.axis_index("dp")
    local_heads = HEADS // tensor_count
    group_heads = HEADS // KV_HEADS
    kv_local = max(1, local_heads // group_heads)
    per_kv = local_heads // kv_local
    kv_width = kv_local * HEAD_DIM
    span_rows = cache_keys.shape[1]
    copies = tensor_count // KV_HEADS

    def spread(cache_block):
        return jnp.repeat(
            cache_block.reshape(GROUP_REQ, span_rows, KV_HEADS, HEAD_DIM), copies, axis=2
        )

    full_keys, full_values = (
        lax.all_to_all(spread(cache_keys), "tensor", split_axis=2, concat_axis=1, tiled=True),
        lax.all_to_all(spread(cache_values), "tensor", split_axis=2, concat_axis=1, tiled=True),
    )
    kv_first = my_rank * local_heads // group_heads
    draft_k = lax.dynamic_slice_in_dim(draft_keys, kv_first * HEAD_DIM, kv_width, 1).reshape(
        GROUP_REQ, DRAFT, kv_local, HEAD_DIM
    )
    draft_v = lax.dynamic_slice_in_dim(draft_values, kv_first * HEAD_DIM, kv_width, 1).reshape(
        GROUP_REQ, DRAFT, kv_local, HEAD_DIM
    )
    local_queries = queries.reshape(GROUP_REQ, DRAFT, kv_local, per_kv, HEAD_DIM)
    my_lengths = lax.dynamic_slice_in_dim(draft_lengths, my_group * GROUP_REQ, GROUP_REQ)
    attended = lax.map(
        attend_one,
        (local_queries, full_keys, full_values, draft_k, draft_v, cache_lengths, my_lengths),
    )
    width_local = local_heads * HEAD_DIM
    attended_rows = attended.reshape(GROUP_REQ * DRAFT, width_local)
    target_rows = PACK * data_count // tensor_count
    home_all = lax.all_gather(attended_rows, "dp", axis=0, tiled=True)
    row_ids = jnp.arange(lax.axis_size("tensor") * target_rows, dtype=jnp.int32)
    request, within, is_live = packed_sources(row_ids, draft_lengths, dest_group, dest_offset)
    picked = jnp.take(home_all, request * DRAFT + within, axis=0)
    picked = jnp.where(is_live[:, None], picked, jnp.zeros((), jnp.bfloat16))
    return lax.psum_scatter(
        jnp.dot(picked, out_weight, preferred_element_type=jnp.float32).astype(jnp.bfloat16),
        "tensor",
        scatter_dimension=0,
        tiled=True,
    )


def solution(mesh):
    in_specs = (
        P("dp", "tensor"),
        P("dp", None),
        P("dp", None),
        P("dp", "tensor", None),
        P("dp", "tensor", None),
        P("tensor", "dp"),
        P("dp"),
        P(),
        P(),
        P(),
    )
    out_specs = P("tensor", "dp")
    return jax.shard_map(body, mesh=mesh, in_specs=in_specs, out_specs=out_specs, check_vma=False)
```

profile of v0, /device:TPU:8, one launch (start us, length us, event | category | flops | bytes accessed | tf_op | source)
XLA Modules:
  0.0 296.0 jit_solution(7023909836648568548)
XLA Ops:
  6.5 1.3 copy_bitcast_fusion.3
  7.9 1.2 broadcast_in_dim.102
  9.1 10.4 %all-to-all-start.1 = ((bf16[2,128,16,128]{3,1,0,2:T(8,128)(2,1)}), bf16[2,128,16,128]{3,1,0,2:T(8,128)(2,1)S(1)}, u32[]{:S(2)}, u32[]{:S(2)}) async-start(bf16[2,128,16,128]{3,1,0,2:T(8,128)(2,1)} %bitcast.25), calls=%async_computation.1 | async-start | bytes 2097152 | tf_op jit(solution)/shard_map/all_to_all | solution.py:94
  19.5 0.1 copy_bitcast_fusion.4
  19.7 26.3 %all-to-all-done.1 = bf16[2,128,16,128]{3,1,0,2:T(8,128)(2,1)S(1)} async-done(((bf16[2,128,16,128]{3,1,0,2:T(8,128)(2,1)}), bf16[2,128,16,128]{3,1,0,2:T(8,128)(2,1)S(1)}, u32[]{:S(2)}, u32[]{:S(2)}) %all-to-all-start.1) | async-done | bytes 1048608 | tf_op jit(solution)/shard_map/all_to_all | solution.py:94
  46.0 1.3 broadcast_in_dim.101
  47.3 5.0 %all-to-all-start = ((bf16[2,128,16,128]{3,1,0,2:T(8,128)(2,1)}), bf16[2,128,16,128]{3,1,0,2:T(8,128)(2,1)}, u32[]{:S(2)}, u32[]{:S(2)}) async-start(bf16[2,128,16,128]{3,1,0,2:T(8,128)(2,1)} %bitcast.20), calls=%async_computation | async-start | bytes 2097152 | tf_op jit(solution)/shard_map/all_to_all | solution.py:95
  52.3 0.0 all-gather.2.cloned.1.call-start
  52.4 0.1 dynamic_slice.34
  52.5 0.8 constant_dynamic-slice_fusion.1
  53.3 0.1 copy.38
  53.4 25.4 %all-to-all-done = bf16[2,128,16,128]{3,1,0,2:T(8,128)(2,1)} async-done(((bf16[2,128,16,128]{3,1,0,2:T(8,128)(2,1)}), bf16[2,128,16,128]{3,1,0,2:T(8,128)(2,1)}, u32[]{:S(2)}, u32[]{:S(2)}) %all-to-all-start) | async-done | bytes 1048608 | tf_op jit(solution)/shard_map/all_to_all | solution.py:95
  78.8 1.3 copy.36
  80.1 14.2 %while.10 = (s32[]{:T(128)}, bf16[2,64,1,8,128]{4,3,1,0,2:T(8,128)(2,1)}, s32[2]{0:T(128)S(1)}, bf16[2,2048,1,128]{3,1,2,0:T(8,128)(2,1)S(1)}, s32[2]{0:T(128)S(...) while((s32[]{:T(128)}, ...), condition=%wide.region_8.9_spmd, body=%wide.region_3.8_spmd.sunk | while | flops 566699072 | bytes 15692581 | solution.py:106
  80.1 0.7 dynamic_slice.73
  80.8 0.7 iota_compare_fusion.6
  81.5 0.7 dynamic_slice.72
  82.2 0.7 iota_compare_fusion.5
  82.9 0.1 fusion.69
  83.0 0.3 fusion.70
  83.2 0.9 bitcast_reduce_fusion.2
  84.1 0.1 fusion.72
  84.2 0.9 fusion.71
  85.1 1.1 fusion.73
  86.2 0.2 fusion.74
  86.5 0.7 copy_dynamic-update-slice_fusion.2
  87.2 0.7 dynamic_slice.73
  87.9 0.7 iota_compare_fusion.6
  88.6 0.7 dynamic_slice.72
  89.3 0.7 iota_compare_fusion.5
  90.0 0.1 fusion.69
  90.0 0.3 fusion.70
  90.3 0.9 bitcast_reduce_fusion.2
  91.2 0.1 fusion.72
  91.3 0.9 fusion.71
  92.2 1.1 fusion.73
  93.3 0.2 fusion.74
  93.6 0.7 copy_dynamic-update-slice_fusion.2
  94.3 1.7 copy.62
  96.0 0.0 all-gather.2.cloned.1.call-update
  96.0 0.0 reduce-scatter.2.cloned.1.call-start
  96.1 0.4 fusion.50
  96.5 0.4 select_reduce_fusion
  96.9 0.1 compare_select_fusion
  97.0 99.9 %all-gather.2.cloned.1.call-done = bf16[4096,1024]{1,0:T(8,128)(2,1)} async-done(((bf16[128,1024]{1,0:T(8,128)(2,1)}), bf16[4096,1024]{1,0:T(8,128)(2,1)}) %all-gather.2.cloned.1.call-update) | async-done | bytes 8388624 | tf_op jit(solution)/shard_map/all_gather | solution.py:113
  196.9 20.4 %gather_fusion = bf16[3072,1024]{1,0:T(8,128)(2,1)} fusion(bf16[4096,1024]{1,0:T(8,128)(2,1)} %all-gather.2.cloned.1.call-done, s32[3072]{0:T(1024)S(1)} %broadcast_clamp_fusion), kind=kCustom, calls=%fused_computation | custom fusion | bytes 12595200 | tf_op jit(solution)/shard_map/jit(_take)/gather | solution.py:116
  217.3 7.6 %fusion.34 = bf16[3072,512]{1,0:T(8,128)(2,1)} fusion(bf16[1024,512]{1,0:T(8,128)(2,1)S(1)} %copy-done, bf16[3072,1024]{1,0:T(8,128)(2,1)} %gather_fusion, pred[3072]{0:T(1024)(128)(4,1)S(1)} %compare_and_fusion.1, pred[3072]{0:T(1024)(128)(4,1)S(1)} %fusion.50), kind=kOutput, calls=%fused_computation.49 | convolution fusion | flops 3229089792 | bytes 10491904 | tf_op jit(solution)/shard_map/dot_general | solution.py:119
  224.9 64.2 %reduce-scatter.2.cloned.1.call-done = bf16[192,512]{1,0:T(8,128)(2,1)} async-done(((bf16[3072,512]{1,0:T(8,128)(2,1)}), bf16[192,512]{1,0:T(8,128)(2,1)}) %reduce-scatter.2.cloned.1.call-update) | async-done | bytes 196624 | tf_op jit(solution)/shard_map/reduce_scatter | solution.py:118
  (28 shorter events, 0.2 us)
Async XLA Ops:
  6.5 210.7 %copy-start = (bf16[1024,512]{1,0:T(8,128)(2,1)S(1)}, bf16[1024,512]{1,0:T(8,128)(2,1)}, u32[]{:S(2)}) copy-start(bf16[1024,512]{1,0:T(8,128)(2,1)} %param.17) | copy-start | bytes 3145732
  6.5 13.0 %copy-start.1 = (bf16[2,128,1024]{2,1,0:T(8,128)(2,1)S(1)}, bf16[2,128,1024]{2,1,0:T(8,128)(2,1)}, u32[]{:S(2)}) copy-start(bf16[2,128,1024]{2,1,0:T(8,128)(2,1)} %param.16) | copy-start | bytes 1572868
  7.8 44.5 %copy-start.2 = (bf16[128,1024]{1,0:T(8,128)(2,1)S(1)}, bf16[128,1024]{1,0:T(8,128)(2,1)}, u32[]{:S(2)}) copy-start(bf16[128,1024]{1,0:T(8,128)(2,1)} %param.12) | copy-start | bytes 786436
  7.8 44.6 %copy-start.6 = (s32[64]{0:T(128)S(1)}, s32[64]{0:T(128)}, u32[]{:S(2)}) copy-start(s32[64]{0:T(128)} %param.19) | copy-start | bytes 772
  9.1 36.9 %all-to-all-start.1 = ((bf16[2,128,16,128]{3,1,0,2:T(8,128)(2,1)}), bf16[2,128,16,128]{3,1,0,2:T(8,128)(2,1)S(1)}, u32[]{:S(2)}, u32[]{:S(2)}) async-start(bf16[2,128,16,128]{3,1,0,2:T(8,128)(2,1)} %bitcast.25), calls=%async_computation.1 | async-start | bytes 2097152 | tf_op jit(solution)/shard_map/all_to_all | solution.py:94
  19.7 60.4 %copy-start.5 = (s32[2]{0:T(128)S(1)}, s32[2]{0:T(128)}, u32[]{:S(2)}) copy-start(s32[2]{0:T(128)} %param.18) | copy-start | bytes 28
  47.3 31.5 %all-to-all-start = ((bf16[2,128,16,128]{3,1,0,2:T(8,128)(2,1)}), bf16[2,128,16,128]{3,1,0,2:T(8,128)(2,1)}, u32[]{:S(2)}, u32[]{:S(2)}) async-start(bf16[2,128,16,128]{3,1,0,2:T(8,128)(2,1)} %bitcast.20), calls=%async_computation | async-start | bytes 2097152 | tf_op jit(solution)/shard_map/all_to_all | solution.py:95
  52.3 144.6 %all-gather.2.cloned.1.call-start = ((), (), s32[]{:S(2)}) async-start(), calls=%async_computation.3 | async-start | bytes 8650752 | tf_op jit(solution)/shard_map/all_gather | solution.py:113
  80.1 16.0 %copy-start.3 = (s32[64]{0:T(128)S(1)}, s32[64]{0:T(128)}, u32[]{:S(2)}) copy-start(s32[64]{0:T(128)} %param.21) | copy-start | bytes 772
  80.1 16.0 %copy-start.4 = (s32[64]{0:T(128)S(1)}, s32[64]{0:T(128)}, u32[]{:S(2)}) copy-start(s32[64]{0:T(128)} %param.20) | copy-start | bytes 772
  96.0 193.2 %reduce-scatter.2.cloned.1.call-start = ((), (), s32[]{:S(2)}) async-start(), calls=%async_computation.4 | async-start | bytes 3342336 | tf_op jit(solution)/shard_map/reduce_scatter | solution.py:118
Sparse Core Ops, SparseCore 0:
  96.1 100.6 all-gather.1
  225.1 64.0 reduce-scatter.1
where the time goes:
time: 297 us; the launch traced here: 296 us
  waiting for transfers between devices  216 us (73%)
  local copies, waits for them, and re-layouts  32.5 us (11%)
  starting transfers between devices  15.5 us (5%)
  between operations  13.6 us (5%)
  matrix products  12.5 us (4%)
  other arithmetic  5.82 us (2%)
    all_gather x1, waiting for transfers between devices, body(): home_all = lax.all_gather(attended_rows, 'dp', axis=0, tiled=True)  99.9 us
    reduce_scatter x1, waiting for transfers between devices, body(): lax.psum_scatter(jnp.dot(picked, out_weight, preferred_element_type=jnp.f...  64.2 us
    all_to_all x1, waiting for transfers between devices, body(): lax.all_to_all(spread(cache_keys), 'tensor', split_axis=2, concat_axis=1,...  26.3 us
    all_to_all x1, waiting for transfers between devices, body(): lax.all_to_all(spread(cache_values), 'tensor', split_axis=2, concat_axis=...  25.4 us
    gather x1, local copies, waits for them, and re-layouts, body(): picked = jnp.take(home_all, request * DRAFT + within, axis=0)  20.4 us
    all_to_all x1, starting transfers between devices, body(): lax.all_to_all(spread(cache_keys), 'tensor', split_axis=2, concat_axis=1,...  10.4 us
    dot_general x1, matrix products, body(): jnp.dot(picked, out_weight, preferred_element_type=jnp.float32)  7.65 us
  transfers between devices with their start and end apart: 4, of which 4 were waited for; matrix products, arithmetic and copies ran while one was open for 1% of the time, Pallas kernels for 0%

commit v1 on v0

--- a/solution.py
+++ b/solution.py
@@ -10,6 +10,14 @@
 GROUP_REQ = 2
 PACK = 96
 NEG_FILL = -1e30
+
+
+def tiled_gather(shard, axis, dim):
+    devices = lax.axis_size(axis)
+    repeats = [devices if d == dim else 1 for d in range(shard.ndim)]
+    return lax.all_to_all(
+        jnp.tile(shard, repeats), axis, split_axis=dim, concat_axis=dim, tiled=True
+    )
 
 
 def packed_sources(row_ids, draft_lengths, dest_group, dest_offset):
@@ -110,7 +118,7 @@
     width_local = local_heads * HEAD_DIM
     attended_rows = attended.reshape(GROUP_REQ * DRAFT, width_local)
     target_rows = PACK * data_count // tensor_count
-    home_all = lax.all_gather(attended_rows, "dp", axis=0, tiled=True)
+    home_all = tiled_gather(attended_rows, "dp", 0)
     row_ids = jnp.arange(lax.axis_size("tensor") * target_rows, dtype=jnp.int32)
     request, within, is_live = packed_sources(row_ids, draft_lengths, dest_group, dest_offset)
     picked = jnp.take(home_all, request * DRAFT + within, axis=0)

time: 297 us -> 408 us (1.37)
  waiting for transfers between devices: 216 us -> 312 us
  starting transfers between devices: 15.5 us -> 25.7 us
  local copies, waits for them, and re-layouts: 32.5 us -> 36.8 us
    all_to_all x0 -> x1, waiting for transfers between devices: none -> 194 us  [tiled_gather(): lax.all_to_all(jnp.tile(shard, repeats), axis, split_axis=dim, concat_axi...]
    all_gather x1 -> x0, waiting for transfers between devices: 99.9 us -> none  [body(): home_all = lax.all_gather(attended_rows, 'dp', axis=0, tiled=True)]
    all_to_all x0 -> x1, starting transfers between devices: none -> 10.3 us  [tiled_gather(): lax.all_to_all(jnp.tile(shard, repeats), axis, split_axis=dim, concat_axi...]
    all_to_all x1, starting transfers between devices: 10.4 us -> 4.93 us  [body(): lax.all_to_all(spread(cache_keys), 'tensor', split_axis=2, concat_axis=1,...]
    all_to_all x1, starting transfers between devices: 4.98 us -> 10.4 us  [body(): lax.all_to_all(spread(cache_values), 'tensor', split_axis=2, concat_axis=...]
    another operation x0 -> x1, local copies, waits for them, and re-layouts: none -> 4.28 us  [tiled_gather(): jnp.tile(shard, repeats)]
    reduce_scatter x1, waiting for transfers between devices: 64.2 us -> 68.4 us  [body(): lax.psum_scatter(jnp.dot(picked, out_weight, preferred_element_type=jnp.f...]
where the time goes in v1:
time: 408 us; the launch traced here: 407 us
  waiting for transfers between devices  312 us (76%)
  local copies, waits for them, and re-layouts  36.8 us (9%)
  starting transfers between devices  25.7 us (6%)
  between operations  13.6 us (3%)
  matrix products  12.5 us (3%)
  other arithmetic  5.83 us (1%)
    all_to_all x1, waiting for transfers between devices, tiled_gather(): lax.all_to_all(jnp.tile(shard, repeats), axis, split_axis=dim, concat_axi...  194 us
    reduce_scatter x1, waiting for transfers between devices, body(): lax.psum_scatter(jnp.dot(picked, out_weight, preferred_element_type=jnp.f...  68.4 us
    all_to_all x1, waiting for transfers between devices, body(): lax.all_to_all(spread(cache_values), 'tensor', split_axis=2, concat_axis=...  26.3 us
    all_to_all x1, waiting for transfers between devices, body(): lax.all_to_all(spread(cache_keys), 'tensor', split_axis=2, concat_axis=1,...  23.5 us
    gather x1, local copies, waits for them, and re-layouts, body(): picked = jnp.take(home_all, request * DRAFT + within, axis=0)  20.4 us
    all_to_all x1, starting transfers between devices, body(): lax.all_to_all(spread(cache_values), 'tensor', split_axis=2, concat_axis=...  10.4 us
    all_to_all x1, starting transfers between devices, tiled_gather(): lax.all_to_all(jnp.tile(shard, repeats), axis, split_axis=dim, concat_axi...  10.3 us
  transfers between devices with their start and end apart: 4, of which 4 were waited for; matrix products, arithmetic and copies ran while one was open for 1% of the time, Pallas kernels for 0%

profile of v1, /device:TPU:8, one launch (start us, length us, event | category | flops | bytes accessed | tf_op | source)
XLA Modules:
  0.0 407.1 jit_solution(17798751463874585295)
XLA Ops:
  6.5 1.3 copy_bitcast_fusion.4
  7.8 1.2 broadcast_in_dim.101
  9.1 10.4 %all-to-all-start = ((bf16[2,128,16,128]{3,1,0,2:T(8,128)(2,1)}), bf16[2,128,16,128]{3,1,0,2:T(8,128)(2,1)S(1)}, u32[]{:S(2)}, u32[]{:S(2)}) async-start(bf16[2,128,16,128]{3,1,0,2:T(8,128)(2,1)} %bitcast.20), calls=%async_computation | async-start | bytes 2097152 | tf_op jit(solution)/shard_map/all_to_all | solution.py:103
  19.5 0.1 copy_bitcast_fusion.3
  19.7 26.3 %all-to-all-done = bf16[2,128,16,128]{3,1,0,2:T(8,128)(2,1)S(1)} async-done(((bf16[2,128,16,128]{3,1,0,2:T(8,128)(2,1)}), bf16[2,128,16,128]{3,1,0,2:T(8,128)(2,1)S(1)}, u32[]{:S(2)}, u32[]{:S(2)}) %all-to-all-start) | async-done | bytes 1048608 | tf_op jit(solution)/shard_map/all_to_all | solution.py:103
  46.0 1.3 broadcast_in_dim.102
  47.3 4.9 %all-to-all-start.1 = ((bf16[2,128,16,128]{3,1,0,2:T(8,128)(2,1)}), bf16[2,128,16,128]{3,1,0,2:T(8,128)(2,1)S(1)}, u32[]{:S(2)}, u32[]{:S(2)}) async-start(bf16[2,128,16,128]{3,1,0,2:T(8,128)(2,1)} %bitcast.163), calls=%async_computation.1 | async-start | bytes 2097152 | tf_op jit(solution)/shard_map/all_to_all | solution.py:102
  52.2 1.0 copy.48
  53.3 0.1 dynamic_slice.34
  53.3 0.8 constant_dynamic-slice_fusion.1
  54.1 1.1 copy.35
  55.2 23.5 %all-to-all-done.1 = bf16[2,128,16,128]{3,1,0,2:T(8,128)(2,1)S(1)} async-done(((bf16[2,128,16,128]{3,1,0,2:T(8,128)(2,1)}), bf16[2,128,16,128]{3,1,0,2:T(8,128)(2,1)S(1)}, u32[]{:S(2)}, u32[]{:S(2)}) %all-to-all-start.1) | async-done | bytes 1048608 | tf_op jit(solution)/shard_map/all_to_all | solution.py:102
  78.7 0.1 copy.37
  78.8 14.2 %while.10 = (s32[]{:T(128)}, bf16[2,64,1,8,128]{4,3,1,0,2:T(8,128)(2,1)}, s32[2]{0:T(128)S(1)}, bf16[2,2048,1,128]{3,1,2,0:T(8,128)(2,1)}, s32[2]{0:T(128)S(1)},...) while((s32[]{:T(128)}, ...), condition=%wide.region_8.9_spmd, body=%wide.region_3.8_spmd.sunk | while | flops 566699072 | bytes 19887412 | solution.py:114
  78.8 0.7 dynamic_slice.72
  79.5 0.7 iota_compare_fusion.5
  80.2 0.9 bitcast_reduce_fusion.2
  81.1 0.7 dynamic_slice.73
  81.8 0.7 iota_compare_fusion.6
  82.5 0.1 fusion.69
  82.5 0.3 fusion.70
  82.8 0.1 fusion.72
  82.9 1.0 fusion.71
  83.8 1.1 fusion.73
  84.9 0.2 fusion.74
  85.2 0.7 copy_dynamic-update-slice_fusion.2
  85.9 0.7 dynamic_slice.72
  86.6 0.7 iota_compare_fusion.5
  87.3 0.9 bitcast_reduce_fusion.2
  88.2 0.7 dynamic_slice.73
  88.9 0.7 iota_compare_fusion.6
  89.6 0.1 fusion.69
  89.6 0.3 fusion.70
  89.9 0.1 fusion.72
  90.0 1.0 fusion.71
  90.9 1.1 fusion.73
  92.0 0.2 fusion.74
  92.3 0.7 copy_dynamic-update-slice_fusion.2
  93.0 1.0 copy.61
  94.0 4.3 %tile.9 = bf16[32,128,1024]{2,1,0:T(8,128)(2,1)} broadcast(bf16[128,1024]{1,0:T(8,128)(2,1)S(1)} %bitcast.165), dimensions={1,2} | broadcast | bytes 8650752 | tf_op jit(solution)/shard_map/tile | solution.py:19
  98.3 10.3 %all-to-all-start.2 = ((bf16[32,128,1024]{2,1,0:T(8,128)(2,1)}), bf16[32,128,1024]{2,1,0:T(8,128)(2,1)}, u32[]{:S(2)}, u32[]{:S(2)}) async-start(bf16[32,128,1024]{2,1,0:T(8,128)(2,1)} %tile.9), calls=%async_computation.2 | async-start | bytes 16777216 | tf_op jit(solution)/shard_map/all_to_all | solution.py:18
  108.8 0.4 fusion.50
  109.1 0.4 select_reduce_fusion
  109.5 0.1 compare_select_fusion
  109.6 194.1 %all-to-all-done.2 = bf16[32,128,1024]{2,1,0:T(8,128)(2,1)} async-done(((bf16[32,128,1024]{2,1,0:T(8,128)(2,1)}), bf16[32,128,1024]{2,1,0:T(8,128)(2,1)}, u32[]{:S(2)}, u32[]{:S(2)}) %all-to-all-start.2) | async-done | bytes 8388640 | tf_op jit(solution)/shard_map/all_to_all | solution.py:18
  303.8 20.4 %gather_fusion = bf16[3072,1024]{1,0:T(8,128)(2,1)} fusion(bf16[4096,1024]{1,0:T(8,128)(2,1)} %bitcast.32, s32[3072]{0:T(1024)S(1)} %broadcast_clamp_fusion), kind=kCustom, calls=%fused_computation | custom fusion | bytes 12595200 | tf_op jit(solution)/shard_map/jit(_take)/gather | solution.py:124
  324.2 7.6 %fusion.34 = bf16[3072,512]{1,0:T(8,128)(2,1)} fusion(bf16[1024,512]{1,0:T(8,128)(2,1)S(1)} %copy-done, bf16[3072,1024]{1,0:T(8,128)(2,1)} %gather_fusion, pred[3072]{0:T(1024)(128)(4,1)S(1)} %compare_and_fusion.1, pred[3072]{0:T(1024)(128)(4,1)S(1)} %fusion.50), kind=kOutput, calls=%fused_computation.49 | convolution fusion | flops 3229089792 | bytes 10491904 | tf_op jit(solution)/shard_map/dot_general | solution.py:127
  331.8 68.4 %reduce-scatter.2.cloned.1.call-done = bf16[192,512]{1,0:T(8,128)(2,1)} async-done(((bf16[3072,512]{1,0:T(8,128)(2,1)}), bf16[192,512]{1,0:T(8,128)(2,1)}) %reduce-scatter.2.cloned.1.call-update) | async-done | bytes 196624 | tf_op jit(solution)/shard_map/reduce_scatter | solution.py:126
  (30 shorter events, 0.2 us)
Async XLA Ops:
  6.5 317.6 %copy-start = (bf16[1024,512]{1,0:T(8,128)(2,1)S(1)}, bf16[1024,512]{1,0:T(8,128)(2,1)}, u32[]{:S(2)}) copy-start(bf16[1024,512]{1,0:T(8,128)(2,1)} %param.17) | copy-start | bytes 3145732
  6.5 13.0 %copy-start.2 = (bf16[2,128,1024]{2,1,0:T(8,128)(2,1)S(1)}, bf16[2,128,1024]{2,1,0:T(8,128)(2,1)}, u32[]{:S(2)}) copy-start(bf16[2,128,1024]{2,1,0:T(8,128)(2,1)} %param.15) | copy-start | bytes 1572868
  7.8 45.4 %copy-start.6 = (s32[64]{0:T(128)S(1)}, s32[64]{0:T(128)}, u32[]{:S(2)}) copy-start(s32[64]{0:T(128)} %param.19) | copy-start | bytes 772
  9.1 36.9 %all-to-all-start = ((bf16[2,128,16,128]{3,1,0,2:T(8,128)(2,1)}), bf16[2,128,16,128]{3,1,0,2:T(8,128)(2,1)S(1)}, u32[]{:S(2)}, u32[]{:S(2)}) async-start(bf16[2,128,16,128]{3,1,0,2:T(8,128)(2,1)} %bitcast.20), calls=%async_computation | async-start | bytes 2097152 | tf_op jit(solution)/shard_map/all_to_all | solution.py:103
  19.6 59.2 %copy-start.5 = (s32[2]{0:T(128)S(1)}, s32[2]{0:T(128)}, u32[]{:S(2)}) copy-start(s32[2]{0:T(128)} %param.18) | copy-start | bytes 28
  47.3 31.4 %all-to-all-start.1 = ((bf16[2,128,16,128]{3,1,0,2:T(8,128)(2,1)}), bf16[2,128,16,128]{3,1,0,2:T(8,128)(2,1)S(1)}, u32[]{:S(2)}, u32[]{:S(2)}) async-start(bf16[2,128,16,128]{3,1,0,2:T(8,128)(2,1)} %bitcast.163), calls=%async_computation.1 | async-start | bytes 2097152 | tf_op jit(solution)/shard_map/all_to_all | solution.py:102
  80.2 3.6 copy-start.1
  87.3 3.6 copy-start.1
  98.3 10.4 %copy-start.3 = (s32[64]{0:T(128)S(1)}, s32[64]{0:T(128)}, u32[]{:S(2)}) copy-start(s32[64]{0:T(128)} %param.21) | copy-start | bytes 772
  98.3 10.5 %copy-start.4 = (s32[64]{0:T(128)S(1)}, s32[64]{0:T(128)}, u32[]{:S(2)}) copy-start(s32[64]{0:T(128)} %param.20) | copy-start | bytes 772
  98.3 205.5 %all-to-all-start.2 = ((bf16[32,128,1024]{2,1,0:T(8,128)(2,1)}), bf16[32,128,1024]{2,1,0:T(8,128)(2,1)}, u32[]{:S(2)}, u32[]{:S(2)}) async-start(bf16[32,128,1024]{2,1,0:T(8,128)(2,1)} %tile.9), calls=%async_computation.2 | async-start | bytes 16777216 | tf_op jit(solution)/shard_map/all_to_all | solution.py:18
  108.7 291.6 %reduce-scatter.2.cloned.1.call-start = ((), (), s32[]{:S(2)}) async-start(), calls=%async_computation.4 | async-start | bytes 3342336 | tf_op jit(solution)/shard_map/reduce_scatter | solution.py:126
Sparse Core Ops, SparseCore 0:
  332.0 68.2 reduce-scatter.1
